TPU v7x, 32 devices: a whole 2x2x4 slice. The times are simulated.
32 devices in a mesh: row: 4 (over z), col: 2 (over y), depth: 4 (over x, core).
Axes of the slice: x: 2, y: 2, z: 4, core: 2. Of those that a mesh axis runs over, the one named last changes fastest.
Arguments:
- factor: float32 [4096, 1536], P(('row', 'col', 'depth')), may hold values from -1 to 4, as said below
- update: float32 [4096, 256], P(('row', 'col', 'depth')), may hold values from -0.375 to 0.375
Outputs:
- new_factor: float32 [4096, 1536], P(('row', 'col', 'depth'))
- new_update: float32 [4096, 256], P(('row', 'col', 'depth'))
Inputs may be any that keep to these rules, and one draw needn't show every extreme that they name: `factor`: zero above the diagonal; each diagonal entry is 1 or more.
All inputs are finite; a program needn't handle non-finite values.
Results may differ from a plain program's by a relative error of at most 0.00013.
Values sent between devices are 32-bit elements; how exact they have to be, the bound alone decides.
A program may use at most 128 MiB of HBM per device.

v0:
```python
import jax
import jax.numpy as jnp
from jax import lax
from jax.sharding import PartitionSpec as P

B = 512
PANELS = 3


def spread(block, axis, owner):
    block = jnp.where(lax.axis_index(axis) == owner, block, jnp.zeros_like(block))
    return lax.psum(block, axis)


def transform(stacked):
    panel_width = stacked.shape[0]
    diag_block = stacked[:, :panel_width]
    v_block = stacked[:, panel_width:]
    update_rank = v_block.shape[1]
    gram_matrix = jnp.dot(stacked, stacked.T, precision=lax.Precision.HIGHEST)
    new_diag = jnp.linalg.cholesky(gram_matrix)
    leading = jax.scipy.linalg.solve_triangular(new_diag, stacked, lower=True)
    coupling = jax.scipy.linalg.solve_triangular(diag_block, v_block, lower=True)
    identity_k = jnp.eye(update_rank, dtype=jnp.float32)
    inner_gram = identity_k + jnp.dot(coupling.T, coupling, precision=lax.Precision.HIGHEST)
    lower_inner = jnp.linalg.cholesky(inner_gram)
    null_basis = jnp.concatenate([-coupling, identity_k], 0)
    second = jax.scipy.linalg.solve_triangular(lower_inner, null_basis.T, lower=True).T
    return jnp.concatenate([leading.T, second], 1)


def on_device(factor, update):
    rows_dev = factor.shape[0]
    row_ids = lax.axis_index(("row", "col", "depth")) * rows_dev + jnp.arange(
        rows_dev, dtype=jnp.int32
    )
    early_slabs = []
    for owner_index in range(PANELS):
        width = (owner_index + 1) * B
        early_slabs.append(
            (
                spread(factor[:, :width], ("row", "col"), owner_index),
                spread(update, ("row", "col"), owner_index),
            )
        )
    for panel_index in range(PANELS):
        panel_start = panel_index * B
        panel_cols = factor[:, panel_start : panel_start + B]
        stacked = jnp.concatenate([panel_cols, update], 1)
        slab_cols, slab_update = early_slabs[panel_index]
        current = jnp.concatenate([slab_cols[:, panel_start : panel_start + B], slab_update], 1)
        diag_rows = lax.all_gather(current, "depth", axis=0, tiled=True)
        rotation = transform(diag_rows)
        for later in range(panel_index + 1, PANELS):
            later_cols, later_update = early_slabs[later]
            joined = jnp.concatenate(
                [later_cols[:, panel_start : panel_start + B], later_update], 1
            )
            early_slabs[later] = (
                later_cols,
                jnp.dot(joined, rotation[:, B:], precision=lax.Precision.HIGHEST),
            )
        moved = jnp.dot(stacked, rotation, precision=lax.Precision.HIGHEST)
        col_ids = panel_start + jnp.arange(B, dtype=jnp.int32)
        new_cols = jnp.where(row_ids[:, None] >= col_ids[None, :], moved[:, :B], jnp.float32(0.0))
        update = jnp.where(row_ids[:, None] >= panel_start, moved[:, B:], update)
        factor = factor.at[:, panel_start : panel_start + B].set(new_cols)
    return (factor, update)


def solution(mesh):
    return jax.shard_map(
        on_device,
        mesh=mesh,
        in_specs=(P(("row", "col", "depth"), None), P(("row", "col", "depth"), None)),
        out_specs=(P(("row", "col", "depth"), None), P(("row", "col", "depth"), None)),
        check_vma=False,
    )
```

profile of v0, /device:TPU:29, one launch (start us, length us, event | category | flops | bytes accessed | tf_op | source)
XLA Modules:
  0.0 1115.1 jit_solution(5682356321159899076)
XLA Ops:
  11.8 99.6 %all-reduce.5.cloned.1.call-done = (f32[128,256]{1,0:T(8,128)}, f32[128,512]{1,0:T(8,128)}, f32[128,256]{1,0:T(8,128)}, f32[128,1024]{1,0:T(8,128)}, f32[128,256]{1,0:T(8,128)}, /*index=5*/f32[128,1536]{1,0:T(8,128)}) async-done(((f32[128,256]{1,0:T(8,128)}, f32[128,512]{1,0:T(8,128)}, f32[128,256]{1,0:T(8,128)}, f32[128,1024]{1,0:T(8,128)}, f32[128,256]{1,0:T(8,128)}, /*index=5*/f32[128,1536]{1,0:T(8,128)}), ...) | async-done | bytes 1966096 | tf_op jit(solution)/shard_map/psum | solution.py:12
  118.8 15.6 %all-gather.4.cloned.1.call-done = f32[512,768]{1,0:T(8,128)} async-done(((f32[128,768]{1,0:T(8,128)}), f32[512,768]{1,0:T(8,128)}) %all-gather.4.cloned.1.call-update) | async-done | bytes 1572880 | tf_op jit(solution)/shard_map/all_gather | solution.py:52
  136.8 11.6 %while.22 = (s32[]{:T(128)}, f32[512,512]{1,0:T(8,128)}, s32[4,2]{0,1:T(2,128)S(1)}, f32[4,128,128]{2,1,0:T(8,128)S(1)}, s32[]{:T(128)}) while((s32[]{:T(128)}, f32[512,512]{1,0:T(8,128)}, s32[4,2]{0,1:T(2,128)S(1)}, f32[4,128,128]{2,1,0:T(8,128)S(1)}, s32[]{:T(128)}) %tuple.194), condition=%wide.while_cond.4, body=%wide.while_body.4.sunk | while | flops 2 | bytes 131189 | solution.py:23
  148.4 39.5 %custom-call.57 = f32[4,128,128]{1,2,0:T(8,128)S(1)} custom-call(f32[4,128,128]{2,1,0:T(8,128)S(1)} %get-tuple-element.105), custom_call_target="InvertDiagBlocksLowerTriangular" | custom-call | tf_op jit(solution)/shard_map/jit(_solve_triangular)/triangular_solve | solution.py:23
  198.1 11.7 %cholesky.560 = f32[128,128]{1,0:T(8,128)S(1)} custom-call(f32[128,128]{1,0:T(8,128)S(1)} %cholesky.786), custom_call_target="Cholesky" | custom-call | tf_op jit(solution)/shard_map/jit(cholesky)/cholesky | solution.py:26
  210.6 9.8 custom-call.58
  223.2 12.1 %cholesky.570 = f32[128,128]{1,0:T(8,128)S(1)} custom-call(f32[128,128]{1,0:T(8,128)S(1)} %convolution_subtract_fusion.29), custom_call_target="Cholesky" | custom-call | tf_op jit(solution)/shard_map/jit(cholesky)/cholesky | solution.py:26
  239.5 5.6 while.23
  245.7 19.7 %custom-call.59 = f32[2,128,128]{1,2,0:T(8,128)S(1)} custom-call(f32[2,128,128]{2,1,0:T(8,128)S(1)} %get-tuple-element.106), custom_call_target="InvertDiagBlocksLowerTriangular" | custom-call | tf_op jit(solution)/shard_map/jit(_solve_triangular)/triangular_solve | solution.py:28
  269.0 3.7 fusion.236
  272.7 2.6 copy.4
  278.6 13.2 %cholesky.492 = f32[128,128]{1,0:T(8,128)} custom-call(f32[128,128]{1,0:T(8,128)} %cholesky.773), custom_call_target="Cholesky" | custom-call | tf_op jit(solution)/shard_map/jit(cholesky)/cholesky | solution.py:21
  295.8 11.3 %custom-call.53 = f32[1,128,128]{1,2,0:T(8,128)} custom-call(f32[1,128,128]{2,1,0:T(8,128)} %get-tuple-element.256), custom_call_target="InvertDiagBlocksLowerTriangular" | custom-call | tf_op jit(solution)/shard_map/jit(cholesky)/cholesky | solution.py:21
  311.6 13.3 %cholesky.511 = f32[128,128]{1,0:T(8,128)} custom-call(f32[128,128]{1,0:T(8,128)} %cholesky.777), custom_call_target="Cholesky" | custom-call | tf_op jit(solution)/shard_map/jit(cholesky)/cholesky | solution.py:21
  326.9 11.3 %custom-call.54 = f32[1,128,128]{1,2,0:T(8,128)} custom-call(f32[1,128,128]{2,1,0:T(8,128)} %get-tuple-element.253), custom_call_target="InvertDiagBlocksLowerTriangular" | custom-call | tf_op jit(solution)/shard_map/jit(cholesky)/cholesky | solution.py:21
  342.8 13.2 %cholesky.532 = f32[128,128]{1,0:T(8,128)} custom-call(f32[128,128]{1,0:T(8,128)} %cholesky.782), custom_call_target="Cholesky" | custom-call | tf_op jit(solution)/shard_map/jit(cholesky)/cholesky | solution.py:21
  357.9 11.5 %custom-call.55 = f32[1,128,128]{1,2,0:T(8,128)} custom-call(f32[1,128,128]{2,1,0:T(8,128)} %get-tuple-element.250), custom_call_target="InvertDiagBlocksLowerTriangular" | custom-call | tf_op jit(solution)/shard_map/jit(cholesky)/cholesky/custom-call.11 | solution.py:21
  373.1 13.2 %cholesky.545 = f32[128,128]{1,0:T(8,128)} custom-call(f32[128,128]{1,0:T(8,128)} %convolution_subtract_fusion.32), custom_call_target="Cholesky" | custom-call | tf_op jit(solution)/shard_map/jit(cholesky)/cholesky | solution.py:21
  396.6 13.6 %while.21 = (s32[]{:T(128)}, f32[512,512]{1,0:T(8,128)}, s32[4,2]{0,1:T(2,128)S(1)}, f32[4,128,128]{2,1,0:T(8,128)}, s32[]{:T(128)}) while((s32[]{:T(128)}, f32[512,512]{1,0:T(8,128)}, s32[4,2]{0,1:T(2,128)S(1)}, f32[4,128,128]{2,1,0:T(8,128)}, s32[]{:T(128)}) %tuple.230), condition=%wide.while_cond.3, body=%wide.while_body.3.sunk | while | flops 2 | bytes 132205 | solution.py:22
  397.2 2.8 bitcast_dynamic-update-slice_fusion.18
  400.7 2.8 bitcast_dynamic-update-slice_fusion.18
  404.1 2.8 bitcast_dynamic-update-slice_fusion.18
  407.5 2.8 bitcast_dynamic-update-slice_fusion.18
  410.3 40.7 %custom-call.56 = f32[4,128,128]{1,2,0:T(8,128)} custom-call(f32[4,128,128]{2,1,0:T(8,128)} %get-tuple-element.104), custom_call_target="InvertDiagBlocksLowerTriangular" | custom-call | tf_op jit(solution)/shard_map/jit(_solve_triangular)/triangular_solve | solution.py:22
  463.8 2.5 fusion
  470.1 4.4 all-gather.6.cloned.1.call-done
  474.5 2.5 slice_select_fusion.1
  477.0 11.6 %while.25 = (s32[]{:T(128)}, f32[512,512]{1,0:T(8,128)}, s32[4,2]{0,1:T(2,128)S(1)}, f32[4,128,128]{2,1,0:T(8,128)S(1)}, s32[]{:T(128)}) while((s32[]{:T(128)}, f32[512,512]{1,0:T(8,128)}, s32[4,2]{0,1:T(2,128)S(1)}, f32[4,128,128]{2,1,0:T(8,128)S(1)}, s32[]{:T(128)}) %tuple.231), condition=%wide.while_cond.4.clone, body=%wide.while_body.4.clone.sunk | while | flops 2 | bytes 131189 | solution.py:23
  488.6 39.5 %custom-call.64 = f32[4,128,128]{1,2,0:T(8,128)S(1)} custom-call(f32[4,128,128]{2,1,0:T(8,128)S(1)} %get-tuple-element.108), custom_call_target="InvertDiagBlocksLowerTriangular" | custom-call | tf_op jit(solution)/shard_map/jit(_solve_triangular)/triangular_solve | solution.py:23
  537.6 11.7 %cholesky.655 = f32[128,128]{1,0:T(8,128)S(1)} custom-call(f32[128,128]{1,0:T(8,128)S(1)} %cholesky.802), custom_call_target="Cholesky" | custom-call | tf_op jit(solution)/shard_map/jit(cholesky)/cholesky | solution.py:26
  549.9 10.4 custom-call.65
  562.5 12.1 %cholesky.665 = f32[128,128]{1,0:T(8,128)S(1)} custom-call(f32[128,128]{1,0:T(8,128)S(1)} %convolution_subtract_fusion.28), custom_call_target="Cholesky" | custom-call | tf_op jit(solution)/shard_map/jit(cholesky)/cholesky | solution.py:26
  578.8 5.3 while.26
  584.1 20.3 %custom-call.66 = f32[2,128,128]{1,2,0:T(8,128)} custom-call(f32[2,128,128]{2,1,0:T(8,128)S(1)} %get-tuple-element.109), custom_call_target="InvertDiagBlocksLowerTriangular" | custom-call | tf_op jit(solution)/shard_map/jit(_solve_triangular)/triangular_solve | solution.py:28
  608.0 2.7 fusion.237
  614.4 11.7 %cholesky.587 = f32[128,128]{1,0:T(8,128)S(1)} custom-call(f32[128,128]{1,0:T(8,128)S(1)} %cholesky.789), custom_call_target="Cholesky" | custom-call | tf_op jit(solution)/shard_map/jit(cholesky)/cholesky | solution.py:21
  626.9 9.8 custom-call.60
  639.9 11.9 %cholesky.606 = f32[128,128]{1,0:T(8,128)S(1)} custom-call(f32[128,128]{1,0:T(8,128)S(1)} %cholesky.793), custom_call_target="Cholesky" | custom-call | tf_op jit(solution)/shard_map/jit(cholesky)/cholesky | solution.py:21
  652.3 9.8 custom-call.61
  665.2 13.2 %cholesky.627 = f32[128,128]{1,0:T(8,128)} custom-call(f32[128,128]{1,0:T(8,128)} %cholesky.798), custom_call_target="Cholesky" | custom-call | tf_op jit(solution)/shard_map/jit(cholesky)/cholesky | solution.py:21
  680.4 11.5 %custom-call.62 = f32[1,128,128]{1,2,0:T(8,128)} custom-call(f32[1,128,128]{2,1,0:T(8,128)} %get-tuple-element.236), custom_call_target="InvertDiagBlocksLowerTriangular" | custom-call | tf_op jit(solution)/shard_map/jit(cholesky)/cholesky/custom-call.11 | solution.py:21
  694.2 11.7 %cholesky.640 = f32[128,128]{1,0:T(8,128)S(1)} custom-call(f32[128,128]{1,0:T(8,128)S(1)} %convolution_subtract_fusion.31), custom_call_target="Cholesky" | custom-call | tf_op jit(solution)/shard_map/jit(cholesky)/cholesky | solution.py:21
  714.2 11.5 %while.24 = (s32[]{:T(128)}, f32[512,512]{1,0:T(8,128)}, s32[4,2]{0,1:T(2,128)S(1)}, f32[4,128,128]{2,1,0:T(8,128)S(1)}, s32[]{:T(128)}) while((s32[]{:T(128)}, f32[512,512]{1,0:T(8,128)}, s32[4,2]{0,1:T(2,128)S(1)}, f32[4,128,128]{2,1,0:T(8,128)S(1)}, s32[]{:T(128)}) %tuple.232), condition=%wide.while_cond.3.clone, body=%wide.while_body.3.clone.sunk | while | flops 2 | bytes 131189 | solution.py:22
  725.7 40.3 %custom-call.63 = f32[4,128,128]{1,2,0:T(8,128)} custom-call(f32[4,128,128]{2,1,0:T(8,128)S(1)} %get-tuple-element.107), custom_call_target="InvertDiagBlocksLowerTriangular" | custom-call | tf_op jit(solution)/shard_map/jit(_solve_triangular)/triangular_solve | solution.py:22
  777.9 2.5 fusion.4
  782.1 6.9 all-gather.8.cloned.1.call-done
  791.1 10.9 while.28
  802.0 40.9 %custom-call.71 = f32[4,128,128]{1,2,0:T(8,128)} custom-call(f32[4,128,128]{2,1,0:T(8,128)} %get-tuple-element.111), custom_call_target="InvertDiagBlocksLowerTriangular" | custom-call | tf_op jit(solution)/shard_map/jit(_solve_triangular)/triangular_solve | solution.py:23
  850.6 11.7 %cholesky.750 = f32[128,128]{1,0:T(8,128)S(1)} custom-call(f32[128,128]{1,0:T(8,128)S(1)} %cholesky.818), custom_call_target="Cholesky" | custom-call | tf_op jit(solution)/shard_map/jit(cholesky)/cholesky | solution.py:26
  864.4 11.3 %custom-call.72 = f32[1,128,128]{1,2,0:T(8,128)} custom-call(f32[1,128,128]{2,1,0:T(8,128)} %get-tuple-element.232), custom_call_target="InvertDiagBlocksLowerTriangular" | custom-call | tf_op jit(solution)/shard_map/jit(cholesky)/cholesky/custom-call.11 | solution.py:26
  878.5 13.6 %cholesky.760 = f32[128,128]{1,0:T(8,128)} custom-call(f32[128,128]{1,0:T(8,128)} %convolution_subtract_fusion.27), custom_call_target="Cholesky" | custom-call | tf_op jit(solution)/shard_map/jit(cholesky)/cholesky | solution.py:26
  897.2 6.5 while.29
  903.7 21.1 %custom-call.73 = f32[2,128,128]{1,2,0:T(8,128)} custom-call(f32[2,128,128]{2,1,0:T(8,128)} %get-tuple-element.112), custom_call_target="InvertDiagBlocksLowerTriangular" | custom-call | tf_op jit(solution)/shard_map/jit(_solve_triangular)/triangular_solve | solution.py:28
  928.5 2.7 fusion.238
  935.0 11.7 %cholesky.682 = f32[128,128]{1,0:T(8,128)S(1)} custom-call(f32[128,128]{1,0:T(8,128)S(1)} %cholesky.805), custom_call_target="Cholesky" | custom-call | tf_op jit(solution)/shard_map/jit(cholesky)/cholesky | solution.py:21
  948.9 11.3 %custom-call.67 = f32[1,128,128]{1,2,0:T(8,128)} custom-call(f32[1,128,128]{2,1,0:T(8,128)} %get-tuple-element.228), custom_call_target="InvertDiagBlocksLowerTriangular" | custom-call | tf_op jit(solution)/shard_map/jit(cholesky)/cholesky | solution.py:21
  964.0 13.3 %cholesky.701 = f32[128,128]{1,0:T(8,128)} custom-call(f32[128,128]{1,0:T(8,128)} %cholesky.809), custom_call_target="Cholesky" | custom-call | tf_op jit(solution)/shard_map/jit(cholesky)/cholesky | solution.py:21
  979.4 11.3 %custom-call.68 = f32[1,128,128]{1,2,0:T(8,128)} custom-call(f32[1,128,128]{2,1,0:T(8,128)} %get-tuple-element.225), custom_call_target="InvertDiagBlocksLowerTriangular" | custom-call | tf_op jit(solution)/shard_map/jit(cholesky)/cholesky | solution.py:21
  994.4 13.2 %cholesky.722 = f32[128,128]{1,0:T(8,128)} custom-call(f32[128,128]{1,0:T(8,128)} %cholesky.814), custom_call_target="Cholesky" | custom-call | tf_op jit(solution)/shard_map/jit(cholesky)/cholesky | solution.py:21
  1009.6 11.4 %custom-call.69 = f32[1,128,128]{1,2,0:T(8,128)} custom-call(f32[1,128,128]{2,1,0:T(8,128)} %get-tuple-element.222), custom_call_target="InvertDiagBlocksLowerTriangular" | custom-call | tf_op jit(solution)/shard_map/jit(cholesky)/cholesky/custom-call.11 | solution.py:21
  1024.0 13.2 %cholesky.735 = f32[128,128]{1,0:T(8,128)} custom-call(f32[128,128]{1,0:T(8,128)} %convolution_subtract_fusion.30), custom_call_target="Cholesky" | custom-call | tf_op jit(solution)/shard_map/jit(cholesky)/cholesky | solution.py:21
  1045.6 11.6 %while.27 = (s32[]{:T(128)}, f32[512,512]{1,0:T(8,128)}, s32[4,2]{0,1:T(2,128)S(1)}, f32[4,128,128]{2,1,0:T(8,128)S(1)}, s32[]{:T(128)}) while((s32[]{:T(128)}, f32[512,512]{1,0:T(8,128)}, s32[4,2]{0,1:T(2,128)S(1)}, f32[4,128,128]{2,1,0:T(8,128)S(1)}, s32[]{:T(128)}) %tuple.234), condition=%wide.while_cond.3.clone.1, body=%wide.while_body.3.clone.1.sunk | while | flops 2 | bytes 131189 | solution.py:22
  1057.2 39.6 %custom-call.70 = f32[4,128,128]{1,2,0:T(8,128)S(1)} custom-call(f32[4,128,128]{2,1,0:T(8,128)S(1)} %get-tuple-element.110), custom_call_target="InvertDiagBlocksLowerTriangular" | custom-call | tf_op jit(solution)/shard_map/jit(_solve_triangular)/triangular_solve | solution.py:22
  1104.7 2.5 fusion.8
  (393 shorter events, 270.9 us)
Async XLA Ops:
  7.2 104.2 %all-reduce.5.cloned.1.call-start = ((), (), s32[]{:S(2)}) async-start(), calls=%async_computation.3 | async-start | bytes 3932160 | tf_op jit(solution)/shard_map/psum | solution.py:12
  8.3 2.6 copy-start.13
  11.8 122.6 %all-gather.4.cloned.1.call-start = ((), (), s32[]{:S(2)}) async-start(), calls=%async_computation | async-start | bytes 1966080 | tf_op jit(solution)/shard_map/all_gather | solution.py:52
  111.4 5.6 copy-start.32
  111.4 6.5 copy-start.25
  113.3 361.2 %all-gather.6.cloned.1.call-start = ((), (), s32[]{:S(2)}) async-start(), calls=%async_computation.1 | async-start | bytes 1966080 | tf_op jit(solution)/shard_map/all_gather | solution.py:52
  113.5 421.2 %copy-start.6 = (f32[256,256]{1,0:T(8,128)}, f32[256,256]{1,0:T(8,128)S(1)}, u32[]{:S(2)}) copy-start(f32[256,256]{1,0:T(8,128)S(1)} %copy.9) | copy-start | bytes 786436
  134.3 53.6 %copy-start = (f32[512,768]{1,0:T(8,128)S(1)}, f32[512,768]{1,0:T(8,128)}, u32[]{:S(2)}) copy-start(f32[512,768]{1,0:T(8,128)} %all-gather.4.cloned.1.call-done) | copy-start | bytes 4718596
  194.6 44.9 %copy-start.46 = (s32[2]{0:T(128)S(1)}, s32[2]{0:T(128)}, u32[]{:S(2)}) copy-start(s32[2]{0:T(128)} %iota_multiply_fusion) | copy-start | bytes 28
  197.4 0.7 copy-start.22
  245.1 0.5 copy-start.45
  265.3 0.7 copy-start.39
  277.0 1.0 copy-start.10
  310.2 0.7 copy-start.26
  341.5 0.7 copy-start.30
  454.7 334.2 %all-gather.8.cloned.1.call-start = ((), (), s32[]{:S(2)}) async-start(), calls=%async_computation.2 | async-start | bytes 1966080 | tf_op jit(solution)/shard_map/all_gather | solution.py:52
  456.5 1.4 copy-start.36
  462.8 1.0 copy-start.20
  463.8 4.0 copy-start.21
  463.8 4.0 copy-start.38
  466.3 3.1 copy-start.44
  474.5 53.6 %copy-start.1 = (f32[512,768]{1,0:T(8,128)S(1)}, f32[512,768]{1,0:T(8,128)}, u32[]{:S(2)}) copy-start(f32[512,768]{1,0:T(8,128)} %all-gather.6.cloned.1.call-done) | copy-start | bytes 4718596
  536.8 0.7 copy-start.23
  575.9 1.9 copy-start.17
  604.4 2.3 copy-start.40
  605.8 0.8 copy-start.4
  613.4 1.0 copy-start.11
  639.2 0.7 copy-start.27
  713.1 53.0 %copy-start.29 = (f32[128,256]{1,0:T(8,128)S(1)}, f32[128,256]{1,0:T(8,128)}, u32[]{:S(2)}) copy-start(f32[128,256]{1,0:T(8,128)} %fusion.47) | copy-start | bytes 393220
  714.2 54.1 %copy-start.19 = (f32[128,512]{1,0:T(8,128)S(1)}, f32[128,512]{1,0:T(8,128)}, u32[]{:S(2)}) copy-start(f32[128,512]{1,0:T(8,128)} %get-tuple-element.209) | copy-start | bytes 786436
  766.1 4.4 copy-start.5
  766.1 4.4 copy-start.8
  770.5 1.4 copy-start.37
  776.8 0.9 copy-start.14
  776.8 1.1 copy-start.15
  777.9 4.1 copy-start.43
  788.9 54.0 %copy-start.2 = (f32[512,768]{1,0:T(8,128)S(1)}, f32[512,768]{1,0:T(8,128)}, u32[]{:S(2)}) copy-start(f32[512,768]{1,0:T(8,128)} %all-gather.8.cloned.1.call-done) | copy-start | bytes 4718596
  842.9 2.9 copy-start.33
  846.2 1.8 copy-start.7
  849.9 0.7 copy-start.24
  862.3 0.6 copy-start.34
  893.6 2.0 copy-start.18
  924.8 2.2 copy-start.41
  934.0 1.0 copy-start.12
  946.7 0.6 copy-start.35
  962.7 0.7 copy-start.28
  993.1 0.7 copy-start.31
  1103.5 1.1 copy-start.9
  1103.6 1.2 copy-start.16
  1104.7 2.6 copy-start.42
  1107.4 0.9 copy-start.3
Sparse Core Ops, SparseCore 0:
  12.9 98.4 all-reduce.4
  113.5 20.7 all-gather.3
  454.8 19.6 all-gather.5
  769.2 19.6 all-gather.7
where the time goes:
time: 1120 us
  other arithmetic  731 us (65%)
  waiting for transfers between devices  126 us (11%)
  local copies, waits for them, and re-layouts  125 us (11%)
  matrix products  105 us (9%)
  between operations  26.8 us (2%)
    another operation x44, other arithmetic, transform(): new_diag = jnp.linalg.cholesky(gram_matrix)  280 us
    another operation x6, other arithmetic, transform(): jax.scipy.linalg.solve_triangular(diag_block, v_block, lower=True)  126 us
    another operation x7, other arithmetic, transform(): leading = jax.scipy.linalg.solve_triangular(new_diag, stacked, lower=True)  125 us
    another operation x20, other arithmetic, transform(): lower_inner = jnp.linalg.cholesky(inner_gram)  111 us
    psum x1, waiting for transfers between devices, spread(): return lax.psum(block, axis)  99.6 us
    another operation x7, other arithmetic, transform(): jax.scipy.linalg.solve_triangular(lower_inner, null_basis.T, lower=True)  65.2 us
    another operation x43, local copies, waits for them, and re-layouts, transform(): leading = jax.scipy.linalg.solve_triangular(new_diag, stacked, lower=True)  38.1 us
    another operation x36, local copies, waits for them, and re-layouts, transform(): jax.scipy.linalg.solve_triangular(diag_block, v_block, lower=True)  33.9 us
  transfers between devices with their start and end apart: 4, of which 4 were waited for; matrix products, arithmetic and copies ran while one was open for 3% of the time, Pallas kernels for 0%

commit v1 on v0

v1 whole, which is shorter than its diff:
```python
import functools

import jax
import jax.numpy as jnp
from jax import lax
from jax.experimental import pallas as pl
from jax.experimental.pallas import tpu as pltpu
from jax.sharding import PartitionSpec as P

B = 512
PANELS = 3
T = 128
S = 16
NN = ((1,), (0,))
NT = ((1,), (1,))
TN = ((0,), (0,))


def split(x):
    high = x.astype(jnp.bfloat16)
    return high, (x - high.astype(jnp.float32)).astype(jnp.bfloat16)


def mms(a, b, dims):
    def dot(p, q):
        return lax.dot_general(p, q, (dims, ((), ())), preferred_element_type=jnp.float32)

    return dot(a[0], b[0]) + (dot(a[0], b[1]) + dot(a[1], b[0]))


def mm(a, b, dims):
    return mms(split(a), split(b), dims)


def invert(ref, count, symmetric):
    sub = lax.broadcasted_iota(jnp.int32, (S, T), 0)
    lane = lax.broadcasted_iota(jnp.int32, (S, T), 1)
    all_lane = lax.broadcasted_iota(jnp.int32, (T, T), 1)
    all_row = lax.broadcasted_iota(jnp.int32, (T, T), 0)

    def body(block, carry):
        first = pl.multiple_of(block * S, S)
        rows = [
            pltpu.roll(ref[m, pl.ds(first, S), :], lax.rem(T - first, T), 1) for m in range(count)
        ]
        diag = [jnp.ones((S, T), jnp.float32) for _ in range(count)]
        for s in range(S):
            for m in range(count):
                r = rows[m]
                col = jnp.broadcast_to(r[:, s : s + 1], (S, T))
                pivot = jnp.broadcast_to(col[s : s + 1, :], (S, T))
                diag[m] = jnp.where(sub == s, pivot, diag[m])
                r = jnp.where((lane == s) & (sub >= s), jnp.where(sub == s, 1.0, 0.0), r)
                scaled = r[s : s + 1, :] / pivot[0:1, :]
                rows[m] = r - jnp.where(sub > s, col, 0.0) * scaled
        in_block = (all_lane >= first) & (all_lane < first + S)
        for m in range(count):
            r = rows[m]
            r = r * lax.rsqrt(diag[m]) if symmetric else r / diag[m]
            r = pltpu.roll(r, first, 1)
            r = jnp.where((lane > sub + first) & (lane < first + S), 0.0, r)
            a = ref[m]
            right = split(r)
            if symmetric:
                left = split(jnp.where(lane >= first + S, r, 0.0))
                change = mms(left, right, TN)
                ref[m] = jnp.where(in_block, 0.0, a) - change
            else:
                left = jnp.where(in_block & (all_row >= first + S), a, 0.0)
                wide = [jnp.where(all_row // S == block, jnp.concatenate([q.astype(jnp.float32)] * (T // S), 0), 0.0).astype(jnp.bfloat16) for q in right]
                change = mms(split(left), wide, NN)
                ref[m] = jnp.where(in_block, 0.0, a) - change
            ref[m, pl.ds(first, S), :] = jnp.where(lane <= sub + first, r, 0.0)
        return carry

    lax.fori_loop(0, T // S, body, 0)


def kernel(start_ref, *refs):
    fs = refs[:PANELS]
    us = refs[PANELS : 2 * PANELS]
    f_ref, u_ref, of_ref, ou_ref = refs[2 * PANELS : 2 * PANELS + 4]
    dinv, w11, w22, w21, tinv_h, tinv_l, sinv, hh, hl, gh, gl = refs[2 * PANELS + 4 :]
    per = B // T
    count = PANELS * per
    rank = u_ref.shape[1]
    half = rank // 2
    eye = jnp.where(
        lax.broadcasted_iota(jnp.int32, (T, T), 0) == lax.broadcasted_iota(jnp.int32, (T, T), 1), 1.0, 0.0
    )

    def blk(j):
        return slice(j * T, (j + 1) * T)

    for j in range(count):
        dinv[j] = fs[j // per][blk(j % per), blk(j)]
    invert(dinv, count, False)

    total = [[eye, None], [jnp.zeros((half, half), jnp.float32), eye]]
    for j in range(count):
        t = us[j // per][blk(j % per), :]
        if j:
            left = split(fs[j // per][blk(j % per), : j * T])
            t = t - mms(left, (hh[: j * T, :], hl[: j * T, :]), NN)
        h = split(mm(dinv[j], t, NN))
        hh[blk(j), :], hl[blk(j), :] = h
        g = mms(h, h, TN)
        total[0][0] = total[0][0] + g[:half, :half]
        total[1][0] = total[1][0] + g[half:, :half]
        total[1][1] = total[1][1] + g[half:, half:]
        w11[j], w21[j], w22[j] = total[0][0], total[1][0], total[1][1]

    invert(w11, count, True)
    for j in range(count):
        low = mm(w21[j], w11[j], NT)
        w21[j] = low
        low = split(low)
        w22[j] = w22[j] - mms(low, low, NT)
    invert(w22, count, True)
    for j in range(count):
        x21 = -mm(w22[j], mm(w21[j], w11[j], NN), NN)
        for out, x11, x2, x22 in zip((tinv_h, tinv_l), split(w11[j]), split(x21), split(w22[j])):
            out[j, :half, :half] = x11
            out[j, :half, half:] = jnp.zeros_like(x11)
            out[j, half:, :half] = x2
            out[j, half:, half:] = x22
    for j in range(count):
        h = (hh[blk(j), :], hl[blk(j), :])
        g = h if j == 0 else split(mms(h, (tinv_h[j - 1], tinv_l[j - 1]), NT))
        gh[blk(j), :], gl[blk(j), :] = g
        sinv[j] = eye + mms(g, g, NT)
    invert(sinv, count, True)

    rows = f_ref.shape[0]
    row_ids = start_ref[0] + lax.broadcasted_iota(jnp.int32, (rows, T), 0)
    lane = lax.broadcasted_iota(jnp.int32, (rows, T), 1)
    res = u_ref[...]
    for j in range(count):
        f = f_ref[:, blk(j)]
        u = split(res)
        if j:
            u = split(mms(u, (tinv_h[j - 1], tinv_l[j - 1]), NT))
        z = f + mms(u, (gh[blk(j), :], gl[blk(j), :]), NT)
        y = mm(z, sinv[j], NT)
        of_ref[:, blk(j)] = jnp.where(row_ids >= lane + j * T, y, 0.0)
        res = res - mms(split(f), (hh[blk(j), :], hl[blk(j), :]), NN)
    last = start_ref[1]
    ou_ref[...] = mms(split(res), (tinv_h[last], tinv_l[last]), NT)


def update_rows(start, slabs, updates, factor, update):
    count = PANELS * B // T
    rank = update.shape[1]
    half = rank // 2
    f32, b16 = jnp.float32, jnp.bfloat16
    vmem = pl.BlockSpec(memory_space=pltpu.VMEM)
    return pl.pallas_call(
        kernel,
        out_shape=(
            jax.ShapeDtypeStruct(factor.shape, f32),
            jax.ShapeDtypeStruct(update.shape, f32),
        ),
        in_specs=[pl.BlockSpec(memory_space=pltpu.SMEM)] + [vmem] * (2 * PANELS + 2),
        out_specs=(vmem, vmem),
        scratch_shapes=[
            pltpu.VMEM((count, T, T), f32),
            pltpu.VMEM((count, half, half), f32),
            pltpu.VMEM((count, half, half), f32),
            pltpu.VMEM((count, half, half), f32),
            pltpu.VMEM((count, rank, rank), b16),
            pltpu.VMEM((count, rank, rank), b16),
            pltpu.VMEM((count, T, T), f32),
            pltpu.VMEM((count * T, rank), b16),
            pltpu.VMEM((count * T, rank), b16),
            pltpu.VMEM((count * T, rank), b16),
            pltpu.VMEM((count * T, rank), b16),
        ],
        compiler_params=pltpu.CompilerParams(vmem_limit_bytes=56 * 1024 * 1024),
    )(start, *slabs, *updates, factor, update)


def spread(block, axis, owner):
    block = jnp.where(lax.axis_index(axis) == owner, block, jnp.zeros_like(block))
    return lax.psum(block, axis)


def on_device(factor, update):
    rows_dev = factor.shape[0]
    row_start = lax.axis_index(("row", "col", "depth")) * rows_dev
    panel = jnp.minimum(row_start // B, PANELS - 1)
    start = jnp.stack([row_start, (panel + 1) * (B // T) - 1]).astype(jnp.int32)
    slabs, updates = [], []
    for owner in range(PANELS):
        width = (owner + 1) * B
        joined = jnp.concatenate([factor[:, :width], update], 1)
        joined = spread(joined, ("row", "col"), owner)
        joined = lax.all_gather(joined, "depth", axis=0, tiled=True)
        slabs.append(joined[:, :width])
        updates.append(joined[:, width:])
    return update_rows(start, slabs, updates, factor, update)


def solution(mesh):
    return jax.shard_map(
        on_device,
        mesh=mesh,
        in_specs=(P(("row", "col", "depth"), None), P(("row", "col", "depth"), None)),
        out_specs=(P(("row", "col", "depth"), None), P(("row", "col", "depth"), None)),
        check_vma=False,
    )
```

time: 1120 us -> 319 us (0.28)
  other arithmetic: 731 us -> 4.57 us
  Pallas kernels: 0 us -> 112 us
  local copies, waits for them, and re-layouts: 125 us -> 14.9 us
  matrix products: 105 us -> 0 us
  waiting for transfers between devices: 126 us -> 172 us
  between operations: 26.8 us -> 13.8 us
    another operation x86 -> x1, other arithmetic: 709 us -> 0.58 us  [on_device(): start = jnp.stack([row_start, (panel + 1) * (B // T) - 1]).astype(jnp.int32)]
    pallas_call x0 -> x1, Pallas kernels: none -> 112 us  [update_rows(): pl.pallas_call(kernel, out_shape=(jax.ShapeDtypeStruct(factor.shape, f32)...]
    another operation x119 -> x0, local copies, waits for them, and re-layouts: 98.4 us -> none  [the longest x43 38.1 us: transform(): leading = jax.scipy.linalg.solve_triangular(new_diag, stacked, lower=True)]
    another operation x75 -> x0, matrix products: 78.2 us -> none  [the longest x18 25.3 us: transform(): new_diag = jnp.linalg.cholesky(gram_matrix)]
    all_gather x3, waiting for transfers between devices: 26.8 us -> 71.3 us  [on_device(): joined = lax.all_gather(joined, 'depth', axis=0, tiled=True)]
    dot_general x12 -> x0, matrix products: 26.7 us -> none  [the longest x3 9.04 us: transform(): gram_matrix = jnp.dot(stacked, stacked.T, precision=lax.Precision.HIGHEST)]
    unnamed x95 -> x2, local copies, waits for them, and re-layouts: 14.3 us -> 0.01 us
    slice x4 -> x10, local copies, waits for them, and re-layouts: 3.19 us -> 14.9 us  [the longest x3 9.28 us: on_device(): slabs.append(joined[:, :width])]
where the time goes in v1:
time: 319 us; the launch traced here: 318 us
  waiting for transfers between devices  172 us (54%)
  Pallas kernels  112 us (35%)
  local copies, waits for them, and re-layouts  14.9 us (5%)
  between operations  13.8 us (4%)
  other arithmetic  4.57 us (1%)
    pallas_call x1, Pallas kernels, update_rows(): pl.pallas_call(kernel, out_shape=(jax.ShapeDtypeStruct(factor.shape, f32)...  112 us
    psum x1, waiting for transfers between devices, spread(): return lax.psum(block, axis)  99.4 us
    all_gather x3, waiting for transfers between devices, on_device(): joined = lax.all_gather(joined, 'depth', axis=0, tiled=True)  71.3 us
    slice x3, local copies, waits for them, and re-layouts, on_device(): slabs.append(joined[:, :width])  9.28 us
  transfers between devices with their start and end apart: 4, of which 4 were waited for; matrix products, arithmetic and copies ran while one was open for 3% of the time, Pallas kernels for 0%

profile of v1, /device:TPU:29, one launch (start us, length us, event | category | flops | bytes accessed | tf_op | source)
XLA Modules:
  0.0 317.6 jit_solution(14507596055164082848)
XLA Ops:
  7.2 0.0 slice-start
  7.2 0.0 slice-start.1
  7.2 0.0 copy-start
  7.2 0.0 all-reduce.3.cloned.1.call-start
  7.3 2.3 maximum_select_fusion
  9.6 0.0 slice-done
  9.6 0.0 copy-done
  9.6 0.8 maximum_select_fusion.2
  10.4 0.0 slice-done.1
  10.4 0.9 maximum_select_fusion.1
  11.3 0.0 all-reduce.3.cloned.1.call-update
  11.3 0.0 all-gather.4.cloned.1.call-start
  11.3 99.4 %all-reduce.3.cloned.1.call-done = (f32[128,768]{1,0:T(8,128)}, f32[128,1280]{1,0:T(8,128)}, f32[128,1792]{1,0:T(8,128)}) async-done(((f32[128,768]{1,0:T(8,128)}, f32[128,1280]{1,0:T(8,128)}, f32[128,1792]{1,0:T(8,128)}), (f32[128,768]{1,0:T(8,128)}, f32[128,1280]{1,0:T(8,128)}, f32[128,1792]{1,0:T(8,128)})) %all-reduce.3.cloned.1.call-update) | async-done | bytes 1966096 | tf_op jit(solution)/shard_map/psum | solution.py:184
  110.7 0.0 all-gather.4.cloned.1.call-update
  110.8 0.0 all-gather.6.cloned.1.call-start
  110.8 0.7 all-gather.6.cloned.1.call-update
  111.5 0.0 all-gather.8.cloned.1.call-start
  111.5 0.5 all-gather.8.cloned.1.call-update
  112.1 0.6 pad_add_fusion.start_ref
  112.7 20.5 %all-gather.4.cloned.1.call-done = f32[512,768]{1,0:T(8,128)} async-done(((f32[128,768]{1,0:T(8,128)}), f32[512,768]{1,0:T(8,128)}) %all-gather.4.cloned.1.call-update) | async-done | bytes 1572880 | tf_op jit(solution)/shard_map/all_gather | solution.py:197
  133.2 1.9 slice.35.refs_3_
  135.0 2.3 slice.32.refs_0_
  137.3 23.0 %all-gather.6.cloned.1.call-done = f32[512,1280]{1,0:T(8,128)} async-done(((f32[128,1280]{1,0:T(8,128)}), f32[512,1280]{1,0:T(8,128)}) %all-gather.6.cloned.1.call-update) | async-done | bytes 2621456 | tf_op jit(solution)/shard_map/all_gather | solution.py:197
  160.3 1.9 slice.36.refs_4_
  162.2 3.2 %slice.33.refs_1_ = f32[512,1024]{1,0:T(8,128)} slice(f32[512,1280]{1,0:T(8,128)} %all-gather.6.cloned.1.call-done), slice={[0:512], [0:1024]} | slice | bytes 4194304 | tf_op jit(solution)/shard_map/slice | solution.py:198
  165.4 27.8 %all-gather.8.cloned.1.call-done = f32[512,1792]{1,0:T(8,128)} async-done(((f32[128,1792]{1,0:T(8,128)}), f32[512,1792]{1,0:T(8,128)}) %all-gather.8.cloned.1.call-update) | async-done | bytes 3670032 | tf_op jit(solution)/shard_map/all_gather | solution.py:197
  193.2 1.9 slice.37.refs_5_
  195.1 3.8 %slice.34.refs_2_ = f32[512,1536]{1,0:T(8,128)} slice(f32[512,1792]{1,0:T(8,128)} %all-gather.8.cloned.1.call-done), slice={[0:512], [0:1536]} | slice | bytes 6291456 | tf_op jit(solution)/shard_map/slice | solution.py:198
  198.9 112.2 %shard_map.41 = (f32[128,1536]{1,0:T(8,128)}, f32[128,256]{1,0:T(8,128)}) custom-call(s32[2]{0:T(128)} %pad_add_fusion.start_ref, f32[512,512]{1,0:T(8,128)} %slice.32.refs_0_, f32[512,1024]{1,0:T(8,128)} %slice.33.refs_1_, f32[512,1536]{1,0:T(8,128)} %slice.34.refs_2_, f32[512,256]{1,0:T(8,128)} %slice.35.refs_3_, f32[512,256]{1,0:T(8,128)} %slice.36.refs_4_, ...), custom_call_target="tpu_custom_call" | custom-call | tf_op jit(solution)/shard_map/pallas_call | solution.py:157
Async XLA Ops:
  7.2 2.4 slice-start
  7.2 3.2 %slice-start.1 = ((f32[128,1536]{1,0:T(8,128)}), f32[128,1024]{1,0:T(8,128)S(1)}, s32[]{:S(2)}) async-start(f32[128,1536]{1,0:T(8,128)} %refs_6_.1), calls=%async_computation.5 | async-start | bytes 1048576 | tf_op jit(solution)/shard_map/slice | solution.py:195
  7.2 2.4 copy-start
  7.2 103.5 %all-reduce.3.cloned.1.call-start = ((), (), s32[]{:S(2)}) async-start(), calls=%async_computation.3 | async-start | bytes 3932160 | tf_op jit(solution)/shard_map/psum | solution.py:184
  11.3 121.9 %all-gather.4.cloned.1.call-start = ((), (), s32[]{:S(2)}) async-start(), calls=%async_computation | async-start | bytes 1966080 | tf_op jit(solution)/shard_map/all_gather | solution.py:197
  110.8 49.5 %all-gather.6.cloned.1.call-start = ((), (), s32[]{:S(2)}) async-start(), calls=%async_computation.1 | async-start | bytes 3276800 | tf_op jit(solution)/shard_map/all_gather | solution.py:197
  111.5 81.7 %all-gather.8.cloned.1.call-start = ((), (), s32[]{:S(2)}) async-start(), calls=%async_computation.2 | async-start | bytes 4587520 | tf_op jit(solution)/shard_map/all_gather | solution.py:197
Sparse Core Ops, SparseCore 0:
  12.5 98.2 all-reduce.2
  112.3 20.8 all-gather.3
  134.7 25.5 all-gather.5
  161.7 31.4 all-gather.7

commit v2 on v1

--- a/solution.py
+++ b/solution.py
@@ -10,6 +10,8 @@
 B = 512
 PANELS = 3
 T = 128
+PIECES = 4
+MESH = pl.DeviceIdType.MESH
 S = 16
 NN = ((1,), (0,))
 NT = ((1,), (1,))
@@ -77,10 +79,9 @@
 
 
 def kernel(start_ref, *refs):
-    fs = refs[:PANELS]
-    us = refs[PANELS : 2 * PANELS]
-    f_ref, u_ref, of_ref, ou_ref = refs[2 * PANELS : 2 * PANELS + 4]
-    dinv, w11, w22, w21, tinv_h, tinv_l, sinv, hh, hl, gh, gl = refs[2 * PANELS + 4 :]
+    xs = refs[:PANELS]
+    f_ref, u_ref, of_ref, ou_ref = refs[PANELS : PANELS + 4]
+    dinv, w11, w22, w21, tinv_h, tinv_l, sinv, hh, hl, gh, gl = refs[PANELS + 4 :]
     per = B // T
     count = PANELS * per
     rank = u_ref.shape[1]
@@ -93,14 +94,14 @@
         return slice(j * T, (j + 1) * T)
 
     for j in range(count):
-        dinv[j] = fs[j // per][blk(j % per), blk(j)]
+        dinv[j] = xs[j // per][blk(j % per), rank + j * T : rank + (j + 1) * T]
     invert(dinv, count, False)
 
     total = [[eye, None], [jnp.zeros((half, half), jnp.float32), eye]]
     for j in range(count):
-        t = us[j // per][blk(j % per), :]
+        t = xs[j // per][blk(j % per), :rank]
         if j:
-            left = split(fs[j // per][blk(j % per), : j * T])
+            left = split(xs[j // per][blk(j % per), rank : rank + j * T])
             t = t - mms(left, (hh[: j * T, :], hl[: j * T, :]), NN)
         h = split(mm(dinv[j], t, NN))
         hh[blk(j), :], hl[blk(j), :] = h
@@ -148,7 +149,7 @@
     ou_ref[...] = mms(split(res), (tinv_h[last], tinv_l[last]), NT)
 
 
-def update_rows(start, slabs, updates, factor, update):
+def update_rows(start, slabs, factor, update):
     count = PANELS * B // T
     rank = update.shape[1]
     half = rank // 2
@@ -160,7 +161,7 @@
             jax.ShapeDtypeStruct(factor.shape, f32),
             jax.ShapeDtypeStruct(update.shape, f32),
         ),
-        in_specs=[pl.BlockSpec(memory_space=pltpu.SMEM)] + [vmem] * (2 * PANELS + 2),
+        in_specs=[pl.BlockSpec(memory_space=pltpu.SMEM)] + [vmem] * (PANELS + 2),
         out_specs=(vmem, vmem),
         scratch_shapes=[
             pltpu.VMEM((count, T, T), f32),
@@ -176,33 +177,152 @@
             pltpu.VMEM((count * T, rank), b16),
         ],
         compiler_params=pltpu.CompilerParams(vmem_limit_bytes=56 * 1024 * 1024),
-    )(start, *slabs, *updates, factor, update)
-
-
-def spread(block, axis, owner):
-    block = jnp.where(lax.axis_index(axis) == owner, block, jnp.zeros_like(block))
-    return lax.psum(block, axis)
-
-
-def on_device(factor, update):
+    )(start, *slabs, factor, update)
+
+
+def send_kernel(sizes, x_ref, *refs):
+    outs = refs[:PANELS]
+    local_sem, col_send, col_recv, row_send, row_recv, depth_send, depth_recv = refs[PANELS:]
+    n_row, n_col, n_depth = sizes
+    r, c, d = (lax.axis_index(name) for name in ("row", "col", "depth"))
+    bits = [1 << b for b in reversed(range(n_depth.bit_length() - 1))]
+    rows_dev = x_ref.shape[0]
+    piece = rows_dev // PIECES
+    barrier = pltpu.get_barrier_semaphore()
+
+    def greet(target):
+        pl.semaphore_signal(barrier, inc=1, device_id=target, device_id_type=MESH)
+
+    for k in range(1, n_col):
+        greet({"col": lax.rem(c + k, n_col)})
+    for bit in bits:
+        greet({"depth": d ^ bit})
+    turns = (1, n_row - 1) if n_row > 1 else ()
+    for k in turns:
+        greet({"row": lax.rem(r + k, n_row)})
+    pl.semaphore_wait(barrier, n_col - 1 + len(bits) + len(turns))
+
+    def part(p, s, owner):
+        return outs[p].at[owner, pl.ds(s * piece, piece), :]
+
+    def remote(ref, send, recv, target):
+        return pltpu.make_async_remote_copy(
+            src_ref=ref, dst_ref=ref, send_sem=send, recv_sem=recv, device_id=target, device_id_type=MESH
+        )
+
+    def local(p, s, q):
+        width = outs[p].shape[2]
+        return pltpu.make_async_copy(x_ref.at[pl.ds(s * piece, piece), :width], part(p, s, d), local_sem.at[q])
+
+    def col_copy(p, s, q, k):
+        return remote(part(p, s, d), col_send.at[q, k], col_recv.at[q], {"col": lax.rem(c + k, n_col)})
+
+    def row_copy(p, s, q, k):
+        return remote(part(p, s, d), row_send.at[q, k], row_recv.at[q], {"row": r + (1 if k else -1)})
+
+    def depth_copy(p, s, q, held, bit):
+        m = held | bit
+        return remote(part(p, s, d ^ held if held else d), depth_send.at[q, m], depth_recv.at[q, m], {"depth": d ^ bit})
+
+    chunks = [(p, s, p * PIECES + s) for p in range(PANELS) for s in range(PIECES)]
+    for p, s, q in chunks:
+        pl.when((r == p // n_col) & (c == p % n_col))(lambda p=p, s=s, q=q: local(p, s, q).start())
+
+    def arrive(p, s, q):
+        home, col = p // n_col, p % n_col
+
+        @pl.when((r == home) & (c == col))
+        def _():
+            local(p, s, q).wait()
+            for k in range(1, n_col):
+                col_copy(p, s, q, k).start()
+
+        @pl.when((r == home) & (c != col))
+        def _():
+            col_copy(p, s, q, 1).wait_recv()
+
+        @pl.when(r != home)
+        def _():
+            row_copy(p, s, q, 0).wait_recv()
+
+        pl.when((r <= home) & (r > 0))(lambda: row_copy(p, s, q, 0).start())
+        pl.when((r >= home) & (r < n_row - 1))(lambda: row_copy(p, s, q, 1).start())
+        if bits:
+            depth_copy(p, s, q, 0, bits[0]).start()
+
+    def level(p, s, q, t):
+        held = [m for m in range(n_depth) if m % bits[t] == 0]
+        for m in held:
+            if m & bits[t]:
+                depth_copy(p, s, q, m ^ bits[t], bits[t]).wait_recv()
+        if t + 1 < len(bits):
+            for m in held:
+                depth_copy(p, s, q, m, bits[t + 1]).start()
+
+    for n in range(len(chunks) + len(bits)):
+        if n < len(chunks):
+            arrive(*chunks[n])
+        for t in range(len(bits)):
+            if 0 <= n - 1 - t < len(chunks):
+                level(*chunks[n - 1 - t], t)
+
+    for p, s, q in chunks:
+        home, col = p // n_col, p % n_col
+
+        @pl.when((r == home) & (c == col))
+        def _():
+            for k in range(1, n_col):
+                col_copy(p, s, q, k).wait_send()
+
+        pl.when((r <= home) & (r > 0))(lambda: row_copy(p, s, q, 0).wait_send())
+        pl.when((r >= home) & (r < n_row - 1))(lambda: row_copy(p, s, q, 1).wait_send())
+        for t, bit in enumerate(bits):
+            for m in range(n_depth):
+                if m % (2 * bit) == 0:
+                    depth_copy(p, s, q, m, bit).wait_send()
+
+
+def collect(sizes, joined):
+    n_row, n_col, n_depth = sizes
+    rows_dev, width = joined.shape
+    rank = width - PANELS * B
+    count = PANELS * PIECES
+    dma = pltpu.SemaphoreType.DMA
+    hbm = pl.BlockSpec(memory_space=pl.ANY)
+    return pl.pallas_call(
+        functools.partial(send_kernel, sizes),
+        out_shape=tuple(
+            jax.ShapeDtypeStruct((n_depth, rows_dev, rank + (p + 1) * B), jnp.float32) for p in range(PANELS)
+        ),
+        in_specs=[pl.BlockSpec(memory_space=pltpu.VMEM)],
+        out_specs=(hbm,) * PANELS,
+        scratch_shapes=[
+            dma((count,)),
+            dma((count, n_col)),
+            dma((count,)),
+            dma((count, 2)),
+            dma((count,)),
+            dma((count, n_depth)),
+            dma((count, n_depth)),
+        ],
+        compiler_params=pltpu.CompilerParams(collective_id=0, has_side_effects=True),
+    )(joined)
+
+
+def on_device(sizes, factor, update):
     rows_dev = factor.shape[0]
     row_start = lax.axis_index(("row", "col", "depth")) * rows_dev
     panel = jnp.minimum(row_start // B, PANELS - 1)
     start = jnp.stack([row_start, (panel + 1) * (B // T) - 1]).astype(jnp.int32)
-    slabs, updates = [], []
-    for owner in range(PANELS):
-        width = (owner + 1) * B
-        joined = jnp.concatenate([factor[:, :width], update], 1)
-        joined = spread(joined, ("row", "col"), owner)
-        joined = lax.all_gather(joined, "depth", axis=0, tiled=True)
-        slabs.append(joined[:, :width])
-        updates.append(joined[:, width:])
-    return update_rows(start, slabs, updates, factor, update)
+    blocks = collect(sizes, jnp.concatenate([update, factor[:, : PANELS * B]], 1))
+    slabs = [block.reshape(B, block.shape[2]) for block in blocks]
+    return update_rows(start, slabs, factor, update)
 
 
 def solution(mesh):
+    sizes = tuple(mesh.shape[name] for name in ("row", "col", "depth"))
     return jax.shard_map(
-        on_device,
+        functools.partial(on_device, sizes),
         mesh=mesh,
         in_specs=(P(("row", "col", "depth"), None), P(("row", "col", "depth"), None)),
         out_specs=(P(("row", "col", "depth"), None), P(("row", "col", "depth"), None)),

time: 319 us -> 203 us (0.64)
  waiting for transfers between devices: 172 us -> 0 us
  Pallas kernels: 112 us -> 198 us
  local copies, waits for them, and re-layouts: 14.9 us -> 0 us
  between operations: 13.8 us -> 0.66 us
    psum x1 -> x0, waiting for transfers between devices: 99.4 us -> none  [spread(): return lax.psum(block, axis)]
    pallas_call x0 -> x1, Pallas kernels: none -> 85.3 us  [collect(): pl.pallas_call(functools.partial(send_kernel, sizes), out_shape=tuple((ja...]
    all_gather x3 -> x0, waiting for transfers between devices: 71.3 us -> none  [on_device(): joined = lax.all_gather(joined, 'depth', axis=0, tiled=True)]
    slice x10 -> x0, local copies, waits for them, and re-layouts: 14.9 us -> none  [the longest x3 9.28 us: on_device(): slabs.append(joined[:, :width])]
    select_n x3 -> x0, other arithmetic: 3.99 us -> none  [spread(): jnp.where(lax.axis_index(axis) == owner, block, jnp.zeros_like(block))]
  transfers between devices with their start and end apart: 4 -> 0, of which waited for: 4 -> 0; matrix products, arithmetic and copies ran while one was open for 3% -> 0% of each run, Pallas kernels for 0% -> 0%
where the time goes in v2:
time: 203 us; the launch traced here: 201 us
  Pallas kernels  198 us (98%)
  other arithmetic  2.79 us (1%)
    pallas_call x1, Pallas kernels, update_rows(): pl.pallas_call(kernel, out_shape=(jax.ShapeDtypeStruct(factor.shape, f32)...  112 us
    pallas_call x1, Pallas kernels, collect(): pl.pallas_call(functools.partial(send_kernel, sizes), out_shape=tuple((ja...  85.3 us

profile of v2, /device:TPU:29, one launch (start us, length us, event | category | flops | bytes accessed | tf_op | source)
XLA Modules:
  0.0 201.1 jit_solution(7960988208959398803)
XLA Ops:
  0.7 0.6 pad_add_fusion.start_ref
  1.2 2.2 %pad_maximum_fusion.x_ref = f32[128,1792]{1,0:T(8,128)} fusion(f32[128,1536]{1,0:T(8,128)} %refs_3_.1, f32[128,256]{1,0:T(8,128)} %refs_4_.1), kind=kLoop, calls=%fused_computation | loop fusion | flops 229376 | bytes 1835008 | tf_op jit(solution)/shard_map/concatenate | solution.py:317
  3.4 85.3 %shard_map.41 = (f32[4,128,768]{2,1,0:T(8,128)}, f32[4,128,1280]{2,1,0:T(8,128)}, f32[4,128,1792]{2,1,0:T(8,128)}) custom-call(f32[128,1792]{1,0:T(8,128)} %pad_maximum_fusion.x_ref), custom_call_target="tpu_custom_call" | custom-call | tf_op jit(solution)/shard_map/pallas_call | solution.py:292
  88.7 112.3 %shard_map.42 = (f32[128,1536]{1,0:T(8,128)}, f32[128,256]{1,0:T(8,128)}) custom-call(s32[2]{0:T(128)} %pad_add_fusion.start_ref, f32[512,768]{1,0:T(8,128)} %bitcast.7, f32[512,1280]{1,0:T(8,128)} %bitcast.6, f32[512,1792]{1,0:T(8,128)} %bitcast.5, f32[128,1536]{1,0:T(8,128)} %refs_3_.1, f32[128,256]{1,0:T(8,128)} %refs_4_.1), custom_call_target="tpu_custom_call" | custom-call | tf_op jit(solution)/shard_map/pallas_call | solution.py:158

commit v3 on v2

--- a/solution.py
+++ b/solution.py
@@ -81,7 +81,7 @@
 def kernel(start_ref, *refs):
     xs = refs[:PANELS]
     f_ref, u_ref, of_ref, ou_ref = refs[PANELS : PANELS + 4]
-    dinv, w11, w22, w21, tinv_h, tinv_l, sinv, hh, hl, gh, gl = refs[PANELS + 4 :]
+    w11, w22, w21, tinv_h, tinv_l, sinv, hh, hl, gh, gl = refs[PANELS + 4 :]
     per = B // T
     count = PANELS * per
     rank = u_ref.shape[1]
@@ -93,17 +93,13 @@
     def blk(j):
         return slice(j * T, (j + 1) * T)
 
-    for j in range(count):
-        dinv[j] = xs[j // per][blk(j % per), rank + j * T : rank + (j + 1) * T]
-    invert(dinv, count, False)
-
     total = [[eye, None], [jnp.zeros((half, half), jnp.float32), eye]]
     for j in range(count):
         t = xs[j // per][blk(j % per), :rank]
         if j:
             left = split(xs[j // per][blk(j % per), rank : rank + j * T])
             t = t - mms(left, (hh[: j * T, :], hl[: j * T, :]), NN)
-        h = split(mm(dinv[j], t, NN))
+        h = split(t)
         hh[blk(j), :], hl[blk(j), :] = h
         g = mms(h, h, TN)
         total[0][0] = total[0][0] + g[:half, :half]
@@ -147,6 +143,29 @@
         res = res - mms(split(f), (hh[blk(j), :], hl[blk(j), :]), NN)
     last = start_ref[1]
     ou_ref[...] = mms(split(res), (tinv_h[last], tinv_l[last]), NT)
+
+
+def solve_kernel(start_ref, f_ref, u_ref, out_ref, dinv):
+    rank = u_ref.shape[1]
+    width = out_ref.shape[1] - rank
+    dinv[0] = f_ref[:, pl.ds(pl.multiple_of(start_ref[2] * T, T), T)]
+    invert(dinv, 1, False)
+    inverse = split(dinv[0])
+    out_ref[:, :rank] = mms(inverse, split(u_ref[...]), NN)
+    for k in range(0, width, T):
+        out_ref[:, rank + k : rank + k + T] = mms(inverse, split(f_ref[:, k : k + T]), NN)
+
+
+def solve_rows(start, factor, update):
+    width = update.shape[1] + PANELS * B - T
+    vmem = pl.BlockSpec(memory_space=pltpu.VMEM)
+    return pl.pallas_call(
+        solve_kernel,
+        out_shape=jax.ShapeDtypeStruct((factor.shape[0], width), jnp.float32),
+        in_specs=[pl.BlockSpec(memory_space=pltpu.SMEM), vmem, vmem],
+        out_specs=vmem,
+        scratch_shapes=[pltpu.VMEM((1, T, T), jnp.float32)],
+    )(start, factor, update)
 
 
 def update_rows(start, slabs, factor, update):
@@ -164,7 +183,6 @@
         in_specs=[pl.BlockSpec(memory_space=pltpu.SMEM)] + [vmem] * (PANELS + 2),
         out_specs=(vmem, vmem),
         scratch_shapes=[
-            pltpu.VMEM((count, T, T), f32),
             pltpu.VMEM((count, half, half), f32),
             pltpu.VMEM((count, half, half), f32),
             pltpu.VMEM((count, half, half), f32),
@@ -218,11 +236,20 @@
         return remote(part(p, s, d), col_send.at[q, k], col_recv.at[q], {"col": lax.rem(c + k, n_col)})
 
     def row_copy(p, s, q, k):
-        return remote(part(p, s, d), row_send.at[q, k], row_recv.at[q], {"row": r + (1 if k else -1)})
+        return remote(part(p, s, d), row_send.at[q, k], row_recv.at[q], {"row": lax.rem(r + (1 if k else n_row - 1), n_row)})
 
     def depth_copy(p, s, q, held, bit):
         m = held | bit
         return remote(part(p, s, d ^ held if held else d), depth_send.at[q, m], depth_recv.at[q, m], {"depth": d ^ bit})
+
+    def row_sends(p):
+        home = p // n_col
+        away = lax.rem(r - home + n_row, n_row)
+        up = n_row // 2 if home % 2 else n_row - 1 - n_row // 2
+        down = n_row - 1 - up
+        sends_up = away < up
+        sends_down = (away == 0) & (down > 0) | (away > n_row - down)
+        return sends_down, sends_up
 
     chunks = [(p, s, p * PIECES + s) for p in range(PANELS) for s in range(PIECES)]
     for p, s, q in chunks:
@@ -245,8 +272,8 @@
         def _():
             row_copy(p, s, q, 0).wait_recv()
 
-        pl.when((r <= home) & (r > 0))(lambda: row_copy(p, s, q, 0).start())
-        pl.when((r >= home) & (r < n_row - 1))(lambda: row_copy(p, s, q, 1).start())
+        for k, sends in enumerate(row_sends(p)):
+            pl.when(sends)(lambda k=k: row_copy(p, s, q, k).start())
         if bits:
             depth_copy(p, s, q, 0, bits[0]).start()
 
@@ -274,8 +301,8 @@
             for k in range(1, n_col):
                 col_copy(p, s, q, k).wait_send()
 
-        pl.when((r <= home) & (r > 0))(lambda: row_copy(p, s, q, 0).wait_send())
-        pl.when((r >= home) & (r < n_row - 1))(lambda: row_copy(p, s, q, 1).wait_send())
+        for k, sends in enumerate(row_sends(p)):
+            pl.when(sends)(lambda k=k: row_copy(p, s, q, k).wait_send())
         for t, bit in enumerate(bits):
             for m in range(n_depth):
                 if m % (2 * bit) == 0:
@@ -285,14 +312,14 @@
 def collect(sizes, joined):
     n_row, n_col, n_depth = sizes
     rows_dev, width = joined.shape
-    rank = width - PANELS * B
+    rank = width - PANELS * B + T
     count = PANELS * PIECES
     dma = pltpu.SemaphoreType.DMA
     hbm = pl.BlockSpec(memory_space=pl.ANY)
     return pl.pallas_call(
         functools.partial(send_kernel, sizes),
         out_shape=tuple(
-            jax.ShapeDtypeStruct((n_depth, rows_dev, rank + (p + 1) * B), jnp.float32) for p in range(PANELS)
+            jax.ShapeDtypeStruct((n_depth, rows_dev, rank + (p + 1) * B - T), jnp.float32) for p in range(PANELS)
         ),
         in_specs=[pl.BlockSpec(memory_space=pltpu.VMEM)],
         out_specs=(hbm,) * PANELS,
@@ -313,8 +340,9 @@
     rows_dev = factor.shape[0]
     row_start = lax.axis_index(("row", "col", "depth")) * rows_dev
     panel = jnp.minimum(row_start // B, PANELS - 1)
-    start = jnp.stack([row_start, (panel + 1) * (B // T) - 1]).astype(jnp.int32)
-    blocks = collect(sizes, jnp.concatenate([update, factor[:, : PANELS * B]], 1))
+    own = jnp.minimum(row_start // T, PANELS * B // T - 1)
+    start = jnp.stack([row_start, (panel + 1) * (B // T) - 1, own]).astype(jnp.int32)
+    blocks = collect(sizes, solve_rows(start, factor, update))
     slabs = [block.reshape(B, block.shape[2]) for block in blocks]
     return update_rows(start, slabs, factor, update)
 

time: 203 us -> 190 us (0.936); the launches traced: 201 us -> 190 us
  Pallas kernels: 198 us -> 189 us
  other arithmetic: 2.79 us -> 0.61 us
    pallas_call x1, Pallas kernels: 112 us -> 81 us  [update_rows(): pl.pallas_call(kernel, out_shape=(jax.ShapeDtypeStruct(factor.shape, f32)...]
    pallas_call x0 -> x1, Pallas kernels: none -> 15.4 us  [solve_rows(): pl.pallas_call(solve_kernel, out_shape=jax.ShapeDtypeStruct((factor.shape...]
    pallas_call x1, Pallas kernels: 85.3 us -> 92.6 us  [collect(): pl.pallas_call(functools.partial(send_kernel, sizes), out_shape=tuple((ja...]
    concatenate x1 -> x0, other arithmetic: 2.21 us -> none  [on_device(): jnp.concatenate([update, factor[:, :PANELS * B]], 1)]
where the time goes in v3:
time: 190 us
  Pallas kernels  189 us (99%)
    pallas_call x1, Pallas kernels, collect(): pl.pallas_call(functools.partial(send_kernel, sizes), out_shape=tuple((ja...  92.6 us
    pallas_call x1, Pallas kernels, update_rows(): pl.pallas_call(kernel, out_shape=(jax.ShapeDtypeStruct(factor.shape, f32)...  81 us
    pallas_call x1, Pallas kernels, solve_rows(): pl.pallas_call(solve_kernel, out_shape=jax.ShapeDtypeStruct((factor.shape...  15.4 us

profile of v3, /device:TPU:29, one launch (start us, length us, event | category | flops | bytes accessed | tf_op | source)
XLA Modules:
  0.0 190.1 jit_solution(10007772712594587771)
XLA Ops:
  0.7 0.6 pad_add_fusion.start_ref
  1.3 15.4 %shard_map.41.x_ref = f32[128,1664]{1,0:T(8,128)} custom-call(s32[3]{0:T(128)} %pad_add_fusion.start_ref, f32[128,1536]{1,0:T(8,128)} %refs_3_.1, f32[128,256]{1,0:T(8,128)} %refs_4_.1), custom_call_target="tpu_custom_call" | custom-call | tf_op jit(solution)/shard_map/pallas_call | solution.py:162
  16.6 92.6 %shard_map.42 = (f32[4,128,640]{2,1,0:T(8,128)}, f32[4,128,1152]{2,1,0:T(8,128)}, f32[4,128,1664]{2,1,0:T(8,128)}) custom-call(f32[128,1664]{1,0:T(8,128)} %shard_map.41.x_ref), custom_call_target="tpu_custom_call" | custom-call | tf_op jit(solution)/shard_map/pallas_call | solution.py:319
  109.2 81.0 %shard_map.43 = (f32[128,1536]{1,0:T(8,128)}, f32[128,256]{1,0:T(8,128)}) custom-call(s32[3]{0:T(128)} %pad_add_fusion.start_ref, f32[512,640]{1,0:T(8,128)} %bitcast.8, f32[512,1152]{1,0:T(8,128)} %bitcast.7, f32[512,1664]{1,0:T(8,128)} %bitcast.6, f32[128,1536]{1,0:T(8,128)} %refs_3_.1, f32[128,256]{1,0:T(8,128)} %refs_4_.1), custom_call_target="tpu_custom_call" | custom-call | tf_op jit(solution)/shard_map/pallas_call | solution.py:177

commit v4 on v3

--- a/solution.py
+++ b/solution.py
@@ -245,7 +245,7 @@
     def row_sends(p):
         home = p // n_col
         away = lax.rem(r - home + n_row, n_row)
-        up = n_row // 2 if home % 2 else n_row - 1 - n_row // 2
+        up = n_row - 1 - home
         down = n_row - 1 - up
         sends_up = away < up
         sends_down = (away == 0) & (down > 0) | (away > n_row - down)

time: 190 us -> 178 us (0.937)
  Pallas kernels: 189 us -> 177 us
    pallas_call x1, Pallas kernels: 92.6 us -> 80.6 us  [collect(): pl.pallas_call(functools.partial(send_kernel, sizes), out_shape=tuple((ja...]
where the time goes in v4:
time: 178 us
  Pallas kernels  177 us (99%)
    pallas_call x1, Pallas kernels, update_rows(): pl.pallas_call(kernel, out_shape=(jax.ShapeDtypeStruct(factor.shape, f32)...  81 us
    pallas_call x1, Pallas kernels, collect(): pl.pallas_call(functools.partial(send_kernel, sizes), out_shape=tuple((ja...  80.6 us
    pallas_call x1, Pallas kernels, solve_rows(): pl.pallas_call(solve_kernel, out_shape=jax.ShapeDtypeStruct((factor.shape...  15.4 us

profile of v4, /device:TPU:29, one launch (start us, length us, event | category | flops | bytes accessed | tf_op | source)
XLA Modules:
  0.0 178.2 jit_solution(8160408101007149107)
XLA Ops:
  0.7 0.6 pad_add_fusion.start_ref
  1.3 15.4 %shard_map.41.x_ref = f32[128,1664]{1,0:T(8,128)} custom-call(s32[3]{0:T(128)} %pad_add_fusion.start_ref, f32[128,1536]{1,0:T(8,128)} %refs_3_.1, f32[128,256]{1,0:T(8,128)} %refs_4_.1), custom_call_target="tpu_custom_call" | custom-call | tf_op jit(solution)/shard_map/pallas_call | solution.py:162
  16.6 80.6 %shard_map.42 = (f32[4,128,640]{2,1,0:T(8,128)}, f32[4,128,1152]{2,1,0:T(8,128)}, f32[4,128,1664]{2,1,0:T(8,128)}) custom-call(f32[128,1664]{1,0:T(8,128)} %shard_map.41.x_ref), custom_call_target="tpu_custom_call" | custom-call | tf_op jit(solution)/shard_map/pallas_call | solution.py:319
  97.2 81.0 %shard_map.43 = (f32[128,1536]{1,0:T(8,128)}, f32[128,256]{1,0:T(8,128)}) custom-call(s32[3]{0:T(128)} %pad_add_fusion.start_ref, f32[512,640]{1,0:T(8,128)} %bitcast.8, f32[512,1152]{1,0:T(8,128)} %bitcast.7, f32[512,1664]{1,0:T(8,128)} %bitcast.6, f32[128,1536]{1,0:T(8,128)} %refs_3_.1, f32[128,256]{1,0:T(8,128)} %refs_4_.1), custom_call_target="tpu_custom_call" | custom-call | tf_op jit(solution)/shard_map/pallas_call | solution.py:177
